TPU v7x, 32 devices: a whole 2x2x4 slice. The times are simulated.
32 devices in a mesh: rows: 8 (over z, x), grp: 4 (over y, core).
Axes of the slice: x: 2, y: 2, z: 4, core: 2. Of those that a mesh axis runs over, the one named last changes fastest.
Arguments:
- tile_values: bfloat16 [1024, 16, 128], P('rows'), may hold values from 0.049804688 to 1
- tile_ids: int32 [1024, 16], P('rows'), may hold values from 0 to 255, as said below
- doc_tiles: int32 [1024], P('rows'), may hold values from 1 to 16
- row_counts: int32 [8], replicated, may hold values from 1 to 128, 512 in all
Outputs:
- similarity: float32 [512, 512], P('rows', 'grp')
Inputs may be any that keep to these rules, and one draw needn't show every extreme that they name: `row_counts`: the entries sum to 512. `tile_ids`: the 16 entries of a row are distinct.
All inputs are finite; a program needn't handle non-finite values.
Results may differ from a plain program's by a relative error of at most 0.0003.
Values may be sent and summed in bfloat16 or wider, within the bound.
A program may use at most 64 MiB of HBM per device.

v0:
```python
import functools

import jax
import jax.numpy as jnp
from jax import lax
from jax.experimental import pallas as pl
from jax.experimental.pallas import tpu as pltpu
from jax.sharding import PartitionSpec as P

MESH = pl.DeviceIdType.MESH
DOC_DEV = 64
ALONG = (((1,), (1,)), ((), ()))


def kernel(R, G, counts_ref, tiles_ref, vals_ref, idblk_ref, out_ref,
           staged, inc_own, inc_peer, place, work, own, own_ids, fold,
           vals, vals_sem, ahead, back, send_sem, recv_sem, give_sem, take_sem, *others):
    cap, K, T = vals_ref.shape
    H = staged.shape[1] - 1
    C = (cap + R - 1) // R
    span = len(others)
    D = DOC_DEV
    me = lax.axis_index("rows")
    grp = lax.axis_index("grp")
    core = lax.rem(grp, 2)
    peer = grp + 1 - 2 * core

    window = vals.shape[0]
    base = jnp.minimum(core * window, cap - window)
    fetch = pltpu.make_async_copy(vals_ref.at[pl.ds(base, window)], vals, vals_sem)
    fetch.start()
    barrier = pltpu.get_barrier_semaphore()

    def greet(d, _):
        pl.semaphore_signal(barrier, inc=1, device_id=(lax.rem(me + d, R), grp),
                            device_id_type=MESH)
        return 0

    lax.fori_loop(1, R, greet, 0)
    pl.semaphore_signal(barrier, inc=1, device_id=(me, peer), device_id_type=MESH)
    order = range(span - 1, -1, -1)

    def distance(i):
        return grp * span + i

    def formed(i):
        k = distance(i)
        return (k == 0) | ((k >= span) & (2 * k <= R)) | (k > R - span)

    def given(i):
        k = distance(i)
        return formed(i) & (k != 0) & (2 * k != R)

    for i in range(span):
        k = R - distance(i)

        @pl.when(jnp.logical_not(formed(i)))
        def _():
            pl.semaphore_signal(barrier, inc=1, device_id=(lax.rem(me + k, R), lax.div(k, span)),
                                device_id_type=MESH)

    def add_up(r, total):
        return total + jnp.where(r < me, counts_ref[r], 0)

    start = lax.fori_loop(0, R, add_up, jnp.int32(0), unroll=R <= 8)
    tile_line = lax.broadcasted_iota(jnp.int32, (K, T), 0)

    def stage(j, _):
        b = lax.rem(j + R - lax.rem(start, R), R)
        for h in range(H):
            s = jnp.minimum((core * H + h) * R + b, cap - 1)
            block = vals[s - base].astype(jnp.float32)
            block = jnp.where(tile_line < tiles_ref[s], block, 0.0)
            staged[j, h] = block.astype(staged.dtype)
        staged[j, H] = idblk_ref[b]
        return 0

    fetch.wait()
    lax.fori_loop(0, R, stage, 0)
    givers = sum(jnp.where(given(i), 1, 0) for i in range(span))
    pl.semaphore_wait(barrier, R + givers)

    def deal(d, _):
        row = lax.rem(me + d, R)
        pltpu.make_async_remote_copy(
            src_ref=staged.at[row], dst_ref=inc_own.at[me],
            send_sem=send_sem.at[0], recv_sem=recv_sem.at[0],
            device_id=(row, grp), device_id_type=MESH).start()
        return 0

    lax.fori_loop(1, R, deal, 0)
    keep = pltpu.make_async_copy(staged.at[me], inc_own.at[me], recv_sem.at[2])
    keep.start()

    def source_of(g):
        def look(r, carry):
            end, behind, begin = carry
            end = end + counts_ref[r]
            past = g >= end
            return (end, behind + jnp.where(past, 1, 0), jnp.where(past, end, begin))

        zero = jnp.int32(0)
        _, source, begin = lax.fori_loop(0, R, look, (zero, zero, zero), unroll=R <= 8)
        return jnp.minimum(source, R - 1), jnp.minimum(lax.div(g - begin, R), C - 1)

    def note(c, _):
        source, a = source_of(c * R + me)
        place[0, c] = source
        place[1, c] = a
        return 0

    lax.fori_loop(0, D, note, 0)

    lane = lax.broadcasted_iota(jnp.int32, (1, T), 1)

    def fill(r, carry):
        begin, line = carry
        count = counts_ref[r]
        b = lax.rem(me + R - lax.rem(begin, R), R)
        slot = (lane - r * C) * R + b
        good = (lane >= r * C) & (lane < r * C + C) & (slot < count)
        return begin + count, jnp.where(good, begin + slot, line)

    nowhere = jnp.full((1, T), -(1 << 30), jnp.int32)
    _, line = lax.fori_loop(0, R, fill, (jnp.int32(0), nowhere), unroll=R <= 8)

    def landing(shift):
        rows = lax.broadcasted_iota(jnp.int32, (2 * D, T), 0) - shift
        return jnp.where(rows * R + me == line, 1.0, 0.0).astype(jnp.bfloat16)

    low, high = landing(0), landing(D)

    keep.wait()
    dealt = pltpu.make_async_remote_copy(
        src_ref=staged.at[pl.ds(0, R - 1)], dst_ref=inc_own.at[pl.ds(0, R - 1)],
        send_sem=send_sem.at[0], recv_sem=recv_sem.at[0],
        device_id=(me, peer), device_id_type=MESH)
    dealt.wait_recv()
    swap = pltpu.make_async_remote_copy(
        src_ref=inc_own, dst_ref=inc_peer,
        send_sem=send_sem.at[1], recv_sem=recv_sem.at[1],
        device_id=(me, peer), device_id_type=MESH)
    swap.start()

    def add_ids(r, total):
        return total + inc_own[r, H].astype(jnp.float32)

    ids = lax.fori_loop(0, R, add_ids, jnp.zeros((K, T), jnp.float32), unroll=R <= 8)
    ids = ids.astype(jnp.bfloat16)
    mine = lax.dot_general(low, ids, ALONG, preferred_element_type=jnp.float32)
    both = [lax.dot_general(ids, hot, ALONG, preferred_element_type=jnp.float32)
            for hot in (low, high)]
    lines = both[0][:K // 2] + both[1][K // 2:]
    own[K * D:K * D + K, :] = jnp.concatenate([lines, lines], axis=0).astype(own.dtype)
    for k in range(K):
        own_ids[k] = jnp.broadcast_to(mine[:D, k:k + 1], (D, T))
    swap.wait_recv()

    def bring(c, _):
        source, a = place[0, c], place[1, c]
        ours = lax.div(a, H) == core
        h = lax.rem(a, H)
        block = jnp.where(ours, inc_own[source, h].astype(jnp.float32),
                          inc_peer[source, h].astype(jnp.float32))
        work[pl.ds(pl.multiple_of(c * K, K), K), :] = block
        return 0

    lax.fori_loop(0, D, bring, 0, unroll=8)
    total = jnp.zeros((D, T), jnp.float32)
    for k in range(K):
        rows = work[pl.ds(k, D, stride=K), :]
        total = total + rows * rows
        own[k * D:(k + 1) * D, :] = rows.astype(own.dtype)
    own_norm = jnp.broadcast_to(jnp.sum(total, axis=1, keepdims=True), (D, T))

    def outgoing(i):
        return pltpu.make_async_remote_copy(
            src_ref=own, dst_ref=others[i],
            send_sem=send_sem.at[2 + i], recv_sem=recv_sem.at[3 + i],
            device_id=(lax.rem(me + grp * span + i, R), grp), device_id_type=MESH)

    first_copy = pltpu.make_async_copy(own, others[0], recv_sem.at[3])

    def when_travels(i, act):
        k = distance(i)

        @pl.when((k != 0) & formed(i))
        def _():
            act(outgoing(i))

    for i in order:
        when_travels(i, lambda copy: copy.start())

    @pl.when(grp == 0)
    def _():
        first_copy.start()

    def giving(i):
        k = distance(i)
        twin = R - k
        j = (span - i) % span
        return pltpu.make_async_remote_copy(
            src_ref=ahead.at[i], dst_ref=back.at[j],
            send_sem=give_sem.at[i], recv_sem=take_sem.at[j],
            device_id=(lax.rem(me + twin, R), lax.div(twin, span)), device_id_type=MESH)

    def compare(i):
        other = others[i]
        fold[...] = other[K * D:K * D + K, :].astype(jnp.float32)

        def norm_part(k, total):
            rows = other[pl.ds(pl.multiple_of(k * D, D), D), :].astype(jnp.float32)
            return total + rows * rows

        total = lax.fori_loop(0, K, norm_part, jnp.zeros((D, T), jnp.float32), unroll=4)
        total = jnp.broadcast_to(jnp.sum(total, axis=1, keepdims=True), (D, T))
        norm = jnp.concatenate([total, total], axis=0).T[:D]

        def step(p, acc):
            parts = [other[pl.ds(pl.multiple_of(k * D, D), D), :]
                     for k in (2 * p, 2 * p + K // 2, 2 * p + 1, 2 * p + 1 + K // 2)]
            block = jnp.concatenate(parts, axis=0)
            marks = [fold[pl.ds(2 * p + i, 1), :] for i in range(2)]
            some = K // 4
            for quarter in range(4):
                rows = own[quarter * some * D:(quarter + 1) * some * D, :]
                gram = lax.dot_general(rows, block, ALONG, preferred_element_type=jnp.float32)
                for kk in range(some):
                    here = own_ids[quarter * some + kk]
                    for i in range(2):
                        part = gram[kk * D:(kk + 1) * D, i * T:(i + 1) * T]
                        acc = acc + jnp.where(here == marks[i], part, 0.0)
            return acc

        acc = lax.fori_loop(0, K // 4, step, jnp.zeros((D, T), jnp.float32))
        product = acc[:, :D] + acc[:, D:2 * D]
        block = product / (own_norm[:, :D] + norm[:, :D] - product)
        wide = jnp.concatenate([block, block], axis=1)
        ahead[i] = jnp.concatenate([wide, wide], axis=0).T[:D]
        out_ref[:, i * D:(i + 1) * D] = block

    for i in order:
        k = distance(i)
        if i == 0:
            @pl.when(grp == 0)
            def _():
                first_copy.wait()

        when_travels(i, lambda copy: copy.wait_recv())

        @pl.when(formed(i))
        def _():
            compare(i)

        @pl.when(given(i))
        def _():
            giving(i).start()

    for i in order:
        k = distance(i)

        @pl.when(jnp.logical_not(formed(i)))
        def _():
            pltpu.make_async_remote_copy(
                src_ref=ahead.at[i], dst_ref=back.at[i],
                send_sem=give_sem.at[i], recv_sem=take_sem.at[i],
                device_id=(me, peer), device_id_type=MESH).wait_recv()
            out_ref[:, i * D:(i + 1) * D] = back[i][:, :D]

        @pl.when(given(i))
        def _():
            giving(i).wait_send()

        when_travels(i, lambda copy: copy.wait_send())

    dealt.wait_send()
    swap.wait_send()


def solution(mesh):
    R, G = mesh.shape["rows"], mesh.shape["grp"]
    span = R // G

    def on_device(tile_values, tile_ids, doc_tiles, row_counts):
        cap, K, T = tile_values.shape
        C = (cap + R - 1) // R
        H = (C + 1) // 2
        me = lax.axis_index("rows")
        ids = jnp.pad(tile_ids, ((0, C * R - cap), (0, 0))).astype(jnp.bfloat16)
        ids = ids.reshape(C, R, K).transpose(1, 2, 0)
        spread = jnp.tile(ids, (1, 1, R))
        spread = jnp.where(jnp.arange(R * C) // C == me, spread, jnp.zeros((), jnp.bfloat16))
        idblk = jnp.pad(spread, ((0, 0), (0, 0), (0, T - R * C)))
        vmem = pl.BlockSpec(memory_space=pltpu.VMEM)
        smem = pl.BlockSpec(memory_space=pltpu.SMEM)
        panel = pltpu.VMEM((DOC_DEV * K + K, T), jnp.bfloat16)
        return pl.pallas_call(
            functools.partial(kernel, R, G),
            out_shape=jax.ShapeDtypeStruct((DOC_DEV, span * DOC_DEV), jnp.float32),
            in_specs=[smem, smem, pl.BlockSpec(memory_space=pl.ANY), vmem],
            out_specs=vmem,
            scratch_shapes=[
                pltpu.VMEM((R, H + 1, K, T), jnp.bfloat16),
                pltpu.VMEM((R, H + 1, K, T), jnp.bfloat16),
                pltpu.VMEM((R, H + 1, K, T), jnp.bfloat16),
                pltpu.SMEM((2, DOC_DEV), jnp.int32),
                pltpu.VMEM((DOC_DEV * K, T), jnp.float32),
                panel,
                pltpu.VMEM((K, DOC_DEV, T), jnp.float32),
                pltpu.VMEM((K, T), jnp.float32),
                pltpu.VMEM((min(H * R, cap), K, T), jnp.bfloat16),
                pltpu.SemaphoreType.DMA,
                pltpu.VMEM((span, DOC_DEV, T), jnp.float32),
                pltpu.VMEM((span, DOC_DEV, T), jnp.float32),
                pltpu.SemaphoreType.DMA((span + 2,)),
                pltpu.SemaphoreType.DMA((span + 3,)),
                pltpu.SemaphoreType.DMA((span,)),
                pltpu.SemaphoreType.DMA((span,)),
            ] + [panel] * span,
            compiler_params=pltpu.CompilerParams(collective_id=0, has_side_effects=True),
        )(row_counts, doc_tiles, tile_values, idblk)

    placed = (P("rows", None, None), P("rows", None), P("rows"), P())
    return jax.shard_map(
        on_device, mesh=mesh, in_specs=placed, out_specs=P("rows", "grp"), check_vma=False
    )
```

profile of v0, /device:TPU:1, one launch (start us, length us, event | category | flops | bytes accessed | tf_op | source)
XLA Modules:
  0.0 35.2 jit_solution(15694640826770456741)
XLA Ops:
  0.0 0.8 %copy.6 = s32[128,16]{1,0:T(8,128)S(1)} copy(s32[128,16]{0,1:T(8,128)} %param.5) | data formatting | bytes 16384 | tf_op args[1]
  0.8 0.1 copy.7
  1.0 0.2 tile.10
  1.2 0.6 %broadcast_select_fusion.idblk_ref = bf16[8,16,128]{2,1,0:T(8,128)(2,1)} fusion(bf16[8,16,128]{2,1,0:T(8,128)(2,1)S(1)} %tile.10, pred[128]{0:T(512)(128)(4,1)S(1)} %fusion), kind=kLoop, calls=%fused_computation.1 | loop fusion | flops 16384 | bytes 65664 | tf_op jit(solution)/shard_map/jit(_where)/select_n | solution.py:292
  1.8 32.0 %shard_map.46 = f32[64,128]{1,0:T(8,128)} custom-call(s32[8]{0:T(128)} %counts_ref.1, s32[128]{0:T(128)} %tiles_ref.1, bf16[128,16,128]{2,1,0:T(8,128)(2,1)} %vals_ref.1, bf16[8,16,128]{2,1,0:T(8,128)(2,1)} %broadcast_select_fusion.idblk_ref), custom_call_target="tpu_custom_call" | custom-call | tf_op jit(solution)/shard_map/pallas_call | solution.py:297
  33.8 1.4 %copy.9 = f32[64,128]{1,0:T(8,128)} copy(f32[64,128]{1,0:T(8,128)} %shard_map.46) | data formatting | bytes 65536
  (3 shorter events, 0.1 us)
where the time goes:
time: 35.5 us; the launch traced here: 35.2 us
  Pallas kernels  32 us (90%)
  local copies, waits for them, and re-layouts  2.5 us (7%)
  other arithmetic  0.64 us (2%)
    pallas_call x1, Pallas kernels, on_device(): pl.pallas_call(functools.partial(kernel, R, G), out_shape=jax.ShapeDtypeS...  32 us
    unnamed x2, local copies, waits for them, and re-layouts  2.17 us

commit v1 on v0

v1 whole, which is shorter than its diff:
```python
import functools

import jax
import jax.numpy as jnp
from jax import lax
from jax.experimental import pallas as pl
from jax.experimental.pallas import tpu as pltpu
from jax.sharding import PartitionSpec as P

MESH = pl.DeviceIdType.MESH
DOC_DEV = 64
ALONG = (((1,), (1,)), ((), ()))


def kernel(R, G, counts_hbm, tiles_hbm, ids_hbm, vals_hbm, num_ref, den_ref,
           counts_ref, tiles_ref, ids, vals, staged, inc, place, work, buf, marks, column,
           id_columns, own_norm, flat, fetch_sem, send_sem, recv_sem, deal_sem):
    cap, K, T = vals.shape
    span = R // G
    D = DOC_DEV
    Q = D // G
    A = staged.shape[1] - 1
    me = lax.axis_index("rows")
    grp = lax.axis_index("grp")
    home = span * G

    fetches = [
        pltpu.make_async_copy(src, dst, fetch_sem.at[n])
        for n, (src, dst) in enumerate(
            ((vals_hbm, vals), (ids_hbm, ids), (counts_hbm, counts_ref), (tiles_hbm, tiles_ref)))
    ]
    for fetch in fetches:
        fetch.start()

    barrier = pltpu.get_barrier_semaphore()

    def greet(row, g):
        pl.semaphore_signal(barrier, inc=1, device_id=(row, g), device_id_type=MESH)

    def greet_row(d, _):
        greet(lax.rem(me + d, R), grp)
        return 0

    lax.fori_loop(1, R, greet_row, 0)
    for e in range(1, G):
        greet(me, lax.rem(grp + e, G))

    def greet_partner(i, _):
        k = grp * span + i

        @pl.when(k != 0)
        def _():
            for g in range(G):
                greet(lax.rem(me + R - k, R), g)

        return 0

    lax.fori_loop(0, span, greet_partner, 0)

    for fetch in fetches[1:]:
        fetch.wait()

    def add_up(r, total):
        return total + jnp.where(r < me, counts_ref[r], 0)

    start = lax.fori_loop(0, R, add_up, jnp.int32(0), unroll=R <= 8)
    tile_line = lax.broadcasted_iota(jnp.int32, (K, T), 0)
    table = ids[...].astype(jnp.float32).astype(staged.dtype)
    fetches[0].wait()

    def stage(b, _):
        lag = lax.rem(start, R * G)
        first = lax.rem(b + R * grp + R * G - lag, R * G)
        for a in range(A):
            s = jnp.minimum(first + a * R * G, cap - 1)
            block = vals[s].astype(jnp.float32)
            block = jnp.where(tile_line < tiles_ref[s], block, 0.0)
            staged[b, a] = block.astype(staged.dtype)
        staged[b, A] = table
        return 0

    lax.fori_loop(0, R, stage, 0)
    pl.semaphore_wait(barrier, 2 * (R - 1) + G - 1)

    def far_first(n):
        half = lax.div(n + 1, 2)
        return R // 2 + jnp.where(lax.rem(n, 2) == 1, half, -half)

    def deal(n, _):
        row = lax.rem(me + far_first(n), R)
        pltpu.make_async_remote_copy(
            src_ref=staged.at[row], dst_ref=inc.at[me],
            send_sem=send_sem.at[0], recv_sem=deal_sem,
            device_id=(row, grp), device_id_type=MESH).start()
        return 0

    lax.fori_loop(0, R - 1, deal, 0)
    inc[me] = staged[me]

    def source_of(g):
        def look(r, carry):
            end, behind, begin = carry
            end = end + counts_ref[r]
            past = g >= end
            return (end, behind + jnp.where(past, 1, 0), jnp.where(past, end, begin))

        zero = jnp.int32(0)
        _, source, begin = lax.fori_loop(0, R, look, (zero, zero, zero), unroll=R <= 8)
        return jnp.minimum(source, R - 1), jnp.minimum(lax.div(g - begin, R * G), A - 1)

    def note(j, _):
        source, a = source_of((j * G + grp) * R + me)
        place[0, j] = source
        place[1, j] = a
        return 0

    lax.fori_loop(0, Q, note, 0)

    dealt = pltpu.make_async_remote_copy(
        src_ref=staged.at[pl.ds(0, R - 1)], dst_ref=inc.at[pl.ds(0, R - 1)],
        send_sem=send_sem.at[0], recv_sem=deal_sem,
        device_id=(me, lax.rem(grp + 1, G)), device_id_type=MESH)
    dealt.wait_recv()

    def bring(j, _):
        work[pl.ds(pl.multiple_of(j * K, K), K), :] = inc[place[0, j], place[1, j]].astype(jnp.float32)
        return 0

    lax.fori_loop(0, Q, bring, 0, unroll=8)
    for k in range(K):
        buf[home + grp, k * Q:(k + 1) * Q, :] = work[pl.ds(k, Q, stride=K), :].astype(buf.dtype)

    def outgoing(slot, row, g):
        return pltpu.make_async_remote_copy(
            src_ref=buf.at[home + grp], dst_ref=buf.at[slot],
            send_sem=send_sem.at[1], recv_sem=recv_sem.at[slot],
            device_id=(row, g), device_id_type=MESH)

    for e in range(1, G):
        outgoing(home + grp, me, lax.rem(grp + e, G)).start()

    def spread(n, _):
        d = far_first(n)
        outgoing(lax.rem(d, span) * G + grp, lax.rem(me + d, R), lax.div(d, span)).start()
        return 0

    lax.fori_loop(0, R - 1, spread, 0)

    lane = lax.broadcasted_iota(jnp.int32, (1, T), 1)
    in_order = jnp.concatenate(
        [(lax.broadcasted_iota(jnp.int32, (Q, T), 0) * G + g) * R for g in range(G)], axis=0)

    def hot(r, begin, panel):
        line = jnp.where(lane < counts_ref[r], begin + lane, -1)
        return jnp.where(in_order + panel == line, 1.0, 0.0).astype(jnp.bfloat16)

    def own_ids(r, carry):
        begin, rows = carry
        rows = rows + lax.dot_general(inc[r, A], hot(r, begin, me), ALONG,
                                      preferred_element_type=jnp.float32)
        return begin + counts_ref[r], rows

    _, rows = lax.fori_loop(0, R, own_ids, (jnp.int32(0), jnp.zeros((K, D), jnp.float32)),
                            unroll=R <= 8)
    marks[...] = jnp.concatenate([rows[:K // 2], rows[K // 2:]], axis=1)

    def partner_ids(i, _):
        panel = lax.rem(me + R - (grp * span + i), R)

        def one(r, carry):
            begin, columns = carry
            columns = columns + lax.dot_general(hot(r, begin, panel), inc[r, A], ALONG,
                                                preferred_element_type=jnp.float32)
            return begin + counts_ref[r], columns

        _, columns = lax.fori_loop(0, R, one, (jnp.int32(0), jnp.zeros((D, K), jnp.float32)),
                                   unroll=R <= 8)
        for k in range(K):
            id_columns[i, k] = jnp.broadcast_to(columns[:, k:k + 1], (D, T))
        return 0

    lax.fori_loop(0, span, partner_ids, 0)

    def arrived(slot):
        return pltpu.make_async_remote_copy(
            src_ref=buf.at[slot], dst_ref=buf.at[slot],
            send_sem=send_sem.at[1], recv_sem=recv_sem.at[slot],
            device_id=(me, lax.rem(grp + 1, G)), device_id_type=MESH)

    def norm_of(slot):
        total = jnp.zeros((Q, T), jnp.float32)
        for k in range(K):
            part = buf[slot, k * Q:(k + 1) * Q, :].astype(jnp.float32)
            total = total + part * part
        return jnp.broadcast_to(jnp.sum(total, axis=1, keepdims=True), (Q, T))

    for g in range(G):
        @pl.when(g != grp)
        def _():
            arrived(home + g).wait_recv()

        own_norm[g * Q:(g + 1) * Q, :] = norm_of(home + g)

    def compare(n, _):
        i = lax.div(n, G)
        g = lax.rem(n, G)
        k = grp * span + i

        @pl.when(k != 0)
        def _():
            arrived(n).wait_recv()

        slot = n + jnp.where(k == 0, home, 0)
        rows = buf[slot]
        sums = [jnp.zeros((Q, T), jnp.float32) for _ in range(2)]
        for p in range(K // 4):
            block = jnp.concatenate(
                [buf[home + h, j * Q:(j + 1) * Q, :]
                 for j in (2 * p, 2 * p + K // 2, 2 * p + 1, 2 * p + 1 + K // 2)
                 for h in range(G)], axis=0)
            gram = lax.dot_general(rows, block, ALONG, preferred_element_type=jnp.float32)
            for j in range(K):
                here = id_columns[i, j, pl.ds(pl.multiple_of(g * Q, Q), Q), :]
                for h in range(2):
                    part = gram[j * Q:(j + 1) * Q, h * T:(h + 1) * T]
                    same = here == marks[2 * p + h:2 * p + h + 1, :]
                    sums[h] = sums[h] + jnp.where(same, part, 0.0)
        total = sums[0] + sums[1]
        total = total + pltpu.roll(total, D, 1)
        flat[pl.ds(i * D + g, Q, stride=G), :] = jnp.where(lane < D, total, norm_of(slot))
        return 0

    lax.fori_loop(0, span * G, compare, 0)

    across = flat[...].T
    for g in range(G):
        product = across[g * Q:(g + 1) * Q]
        rest = own_norm[g * Q:(g + 1) * Q, :1] + across[D + g * Q:D + (g + 1) * Q] - product
        for c in range(span * D // T):
            num_ref[c, pl.ds(g, Q, stride=G), :] = product[:, c * T:(c + 1) * T]
            den_ref[c, pl.ds(g, Q, stride=G), :] = rest[:, c * T:(c + 1) * T]

    dealt.wait_send()
    pltpu.make_async_remote_copy(
        src_ref=buf.at[pl.ds(0, R + G - 2)], dst_ref=buf.at[pl.ds(0, R + G - 2)],
        send_sem=send_sem.at[1], recv_sem=recv_sem.at[0],
        device_id=(me, lax.rem(grp + 1, G)), device_id_type=MESH).wait_send()


def solution(mesh):
    R, G = mesh.shape["rows"], mesh.shape["grp"]
    span = R // G

    def on_device(tile_values, tile_ids, doc_tiles, row_counts):
        cap, K, T = tile_values.shape
        A = (cap + R * G - 1) // (R * G)
        Q = DOC_DEV // G
        anywhere = pl.BlockSpec(memory_space=pl.ANY)
        vmem = pl.BlockSpec(memory_space=pltpu.VMEM)
        part = pltpu.VMEM((span * DOC_DEV // T, DOC_DEV, T), jnp.float32)
        num, den = pl.pallas_call(
            functools.partial(kernel, R, G),
            out_shape=(part, part),
            in_specs=[anywhere] * 4,
            out_specs=(vmem, vmem),
            scratch_shapes=[
                pltpu.SMEM((R,), jnp.int32),
                pltpu.SMEM((cap,), jnp.int32),
                pltpu.VMEM((K, cap), jnp.int32),
                pltpu.VMEM((cap, K, T), jnp.bfloat16),
                pltpu.VMEM((R, A + 1, K, T), jnp.bfloat16),
                pltpu.VMEM((R, A + 1, K, T), jnp.bfloat16),
                pltpu.SMEM((2, Q), jnp.int32),
                pltpu.VMEM((Q * K, T), jnp.float32),
                pltpu.VMEM(((span + 1) * G, K * Q, T), jnp.bfloat16),
                pltpu.VMEM((K // 2, T), jnp.float32),
                pltpu.VMEM((DOC_DEV, T), jnp.float32),
                pltpu.VMEM((span, K, DOC_DEV, T), jnp.float32),
                pltpu.VMEM((DOC_DEV, T), jnp.float32),
                pltpu.VMEM((span * DOC_DEV, T), jnp.float32),
                pltpu.SemaphoreType.DMA((4,)),
                pltpu.SemaphoreType.DMA((2,)),
                pltpu.SemaphoreType.DMA(((span + 1) * G,)),
                pltpu.SemaphoreType.DMA,
            ],
            compiler_params=pltpu.CompilerParams(collective_id=0, has_side_effects=True),
        )(row_counts, doc_tiles, tile_ids.T, tile_values)
        return (num / den).transpose(1, 0, 2).reshape(DOC_DEV, span * DOC_DEV)

    placed = (P("rows", None, None), P("rows", None), P("rows"), P())
    return jax.shard_map(
        on_device, mesh=mesh, in_specs=placed, out_specs=P("rows", "grp"), check_vma=False
    )
```

time: 35.5 us -> 26.8 us (0.75)
  Pallas kernels: 32 us -> 25.7 us
  local copies, waits for them, and re-layouts: 2.5 us -> 0 us
    pallas_call x1, Pallas kernels: 32 us -> 25.7 us  [on_device(): pl.pallas_call(functools.partial(kernel, R, G), out_shape=(part, part), i...]
    unnamed x2 -> x0, local copies, waits for them, and re-layouts: 2.17 us -> none
    another operation x0 -> x1, other arithmetic: none -> 0.63 us  [on_device(): return (num / den).transpose(1, 0, 2).reshape(DOC_DEV, span * DOC_DEV)]
    select_n x1 -> x0, other arithmetic: 0.62 us -> none  [on_device(): jnp.where(jnp.arange(R * C) // C == me, spread, jnp.zeros((), jnp.bfloat16))]
where the time goes in v1:
time: 26.8 us; the launch traced here: 26.4 us
  Pallas kernels  25.7 us (96%)
  other arithmetic  0.63 us (2%)
    pallas_call x1, Pallas kernels, on_device(): pl.pallas_call(functools.partial(kernel, R, G), out_shape=(part, part), i...  25.7 us
    another operation x1, other arithmetic, on_device(): return (num / den).transpose(1, 0, 2).reshape(DOC_DEV, span * DOC_DEV)  0.63 us

profile of v1, /device:TPU:1, one launch (start us, length us, event | category | flops | bytes accessed | tf_op | source)
XLA Modules:
  0.0 26.4 jit_solution(12476261098076458354)
XLA Ops:
  0.0 25.7 %shard_map.46 = (f32[1,64,128]{2,1,0:T(8,128)S(1)}, f32[1,64,128]{2,1,0:T(8,128)S(1)}) custom-call(s32[8]{0:T(128)} %counts_hbm.1, s32[128]{0:T(128)} %tiles_hbm.1, s32[16,128]{1,0:T(8,128)} %bitcast.3, bf16[128,16,128]{2,1,0:T(8,128)(2,1)} %vals_hbm.1), custom_call_target="tpu_custom_call" | custom-call | tf_op jit(solution)/shard_map/pallas_call | solution.py:261
  25.7 0.6 %divide_bitcast_fusion = f32[64,128]{1,0:T(8,128)} fusion(f32[1,64,128]{2,1,0:T(8,128)S(1)} %get-tuple-element.7, f32[1,64,128]{2,1,0:T(8,128)S(1)} %get-tuple-element.8), kind=kLoop, calls=%fused_computation | loop fusion | flops 8192 | bytes 98304 | tf_op jit(solution)/shard_map/reshape;transpose | solution.py:288

commit v2 on v1

v2 whole, which is shorter than its diff:
```python
import functools

import jax
import jax.numpy as jnp
from jax import lax
from jax.experimental import pallas as pl
from jax.experimental.pallas import tpu as pltpu
from jax.sharding import PartitionSpec as P

MESH = pl.DeviceIdType.MESH
DOC_DEV = 64
ALONG = (((1,), (1,)), ((), ()))


def kernel(R, G, counts_hbm, tiles_hbm, ids_hbm, vals_hbm, num_ref, den_ref,
           counts_ref, tiles_ref, ids, vals, staged, inc, place, work, buf, own_columns, id_rows,
           own_norm, squares, parts, fold, fetch_sem, send_sem, spread_sem, recv_sem, deal_sem):
    cap, K, T = vals.shape
    span = R // G
    D = DOC_DEV
    Q = D // G
    A = staged.shape[1] - 1
    me = lax.axis_index("rows")
    grp = lax.axis_index("grp")
    peer = grp + 1 - 2 * lax.rem(grp, 2)
    home = span * G
    levels = R // 2
    level = lax.div(me, 2)
    side = lax.rem(me, 2)

    fetches = [
        pltpu.make_async_copy(src, dst, fetch_sem.at[n])
        for n, (src, dst) in enumerate(
            ((vals_hbm, vals), (ids_hbm, ids), (counts_hbm, counts_ref), (tiles_hbm, tiles_ref)))
    ]
    for fetch in fetches:
        fetch.start()

    barrier = pltpu.get_barrier_semaphore()

    def greet(row, g):
        pl.semaphore_signal(barrier, inc=1, device_id=(row, g), device_id_type=MESH)

    def greet_row(d, _):
        greet(lax.rem(me + d, R), peer)
        return 0

    lax.fori_loop(1, R, greet_row, 0)
    for e in range(1, G):
        greet(me, lax.rem(grp + e, G))

    for fetch in fetches[1:]:
        fetch.wait()

    def add_up(r, total):
        return total + jnp.where(r < me, counts_ref[r], 0)

    start = lax.fori_loop(0, R, add_up, jnp.int32(0), unroll=R <= 8)
    tile_line = lax.broadcasted_iota(jnp.int32, (K, T), 0)
    table = ids[...].astype(jnp.float32).astype(staged.dtype)
    fetches[0].wait()

    def stage(b, _):
        lag = lax.rem(start, R * G)
        first = lax.rem(b + R * jnp.where(b == me, grp, peer) + R * G - lag, R * G)
        for a in range(A):
            s = jnp.minimum(first + a * R * G, cap - 1)
            block = vals[s].astype(jnp.float32)
            block = jnp.where(tile_line < tiles_ref[s], block, 0.0)
            staged[b, a] = block.astype(staged.dtype)
        staged[b, A] = table
        return 0

    lax.fori_loop(0, R, stage, 0)
    pl.semaphore_wait(barrier, R - 1 + G - 1)

    def far_first(n, at, size):
        near = jnp.minimum(at, size - 1 - at)
        m = n - jnp.abs(size - 1 - 2 * at)
        up = jnp.where(m < 0, 2 * at < size, lax.rem(m, 2) == 0)
        away = jnp.where(m < 0, near - m, near - lax.div(m, 2))
        return at + jnp.where(up, away, -away)

    def deal(n, _):
        row = far_first(n, me, R)
        pltpu.make_async_remote_copy(
            src_ref=staged.at[row], dst_ref=inc.at[me],
            send_sem=send_sem, recv_sem=deal_sem,
            device_id=(row, peer), device_id_type=MESH).start()
        return 0

    lax.fori_loop(0, R - 1, deal, 0)
    inc[me] = staged[me]

    def source_of(g):
        def look(r, carry):
            end, behind, begin = carry
            end = end + counts_ref[r]
            past = g >= end
            return (end, behind + jnp.where(past, 1, 0), jnp.where(past, end, begin))

        zero = jnp.int32(0)
        _, source, begin = lax.fori_loop(0, R, look, (zero, zero, zero), unroll=R <= 8)
        return jnp.minimum(source, R - 1), jnp.minimum(lax.div(g - begin, R * G), A - 1)

    def note(j, _):
        source, a = source_of((j * G + grp) * R + me)
        place[0, j] = source
        place[1, j] = a
        return 0

    lax.fori_loop(0, Q, note, 0)

    dealt = pltpu.make_async_remote_copy(
        src_ref=staged.at[pl.ds(0, R - 1)], dst_ref=inc.at[pl.ds(0, R - 1)],
        send_sem=send_sem, recv_sem=deal_sem,
        device_id=(me, lax.rem(grp + 1, G)), device_id_type=MESH)
    dealt.wait_recv()

    def bring(j, _):
        work[pl.ds(pl.multiple_of(j * K, K), K), :] = inc[place[0, j], place[1, j]].astype(jnp.float32)
        return 0

    lax.fori_loop(0, Q, bring, 0, unroll=8)
    for k in range(K):
        buf[home + grp, k * Q:(k + 1) * Q, :] = work[pl.ds(k, Q, stride=K), :].astype(buf.dtype)

    def outgoing(sem, slot, row, g):
        return pltpu.make_async_remote_copy(
            src_ref=buf.at[home + grp], dst_ref=buf.at[slot],
            send_sem=spread_sem.at[sem], recv_sem=recv_sem.at[slot],
            device_id=(row, g), device_id_type=MESH)

    def to_own(e):
        return outgoing(2 * levels + e, home + grp, me, lax.rem(grp + e, G))

    def to_row(sem, row):
        k = lax.rem(row + R - me, R)
        return outgoing(sem, lax.rem(k, span) * G + grp, row, lax.div(k, span))

    def to_level(n, act):
        there = far_first(n, level, levels)
        act(to_row(n, 2 * there + side))

        @pl.when(lax.rem(grp, 2) == 1)
        def _():
            act(to_row(levels + n, 2 * there + 1 - side))

    def spread(act):
        for e in range(1, G):
            act(to_own(e))

        def each(n, _):
            to_level(n, act)
            return 0

        lax.fori_loop(0, levels - 1, each, 0)
        act(to_row(2 * levels, 2 * level + 1 - side))

    spread(lambda copy: copy.start())

    lane = lax.broadcasted_iota(jnp.int32, (1, T), 1)
    in_order = jnp.concatenate(
        [(lax.broadcasted_iota(jnp.int32, (Q, T), 0) * G + g) * R for g in range(G)], axis=0)

    def hot(r, begin, panel):
        line = jnp.where(lane < counts_ref[r], begin + lane, -1)
        return jnp.where(in_order + panel == line, 1.0, 0.0).astype(jnp.bfloat16)

    def own_ids(r, carry):
        begin, columns = carry
        columns = columns + lax.dot_general(hot(r, begin, me), inc[r, A], ALONG,
                                            preferred_element_type=jnp.float32)
        return begin + counts_ref[r], columns

    _, columns = lax.fori_loop(0, R, own_ids, (jnp.int32(0), jnp.zeros((D, K), jnp.float32)),
                               unroll=R <= 8)
    for k in range(K):
        own_columns[k] = jnp.broadcast_to(columns[:, k:k + 1], (D, T))

    within = jnp.concatenate([lax.broadcasted_iota(jnp.int32, (Q, D), 0)] * (T // Q), axis=0)
    low_of = lax.broadcasted_iota(jnp.int32, (K // 2, T), 0) * Q
    lanes = lax.broadcasted_iota(jnp.int32, (K // 2, T), 1)
    in_place = (lanes >= low_of) & (lanes < low_of + Q)

    def partner_ids(i, _):
        panel = lax.rem(me + R - (grp * span + i), R)

        def one(r, carry):
            begin, rows = carry
            rows = rows + lax.dot_general(inc[r, A], hot(r, begin, panel), ALONG,
                                          preferred_element_type=jnp.float32)
            return begin + counts_ref[r], rows

        _, rows = lax.fori_loop(0, R, one, (jnp.int32(0), jnp.zeros((K, D), jnp.float32)),
                                unroll=R <= 8)
        rows = rows.astype(jnp.bfloat16)
        for g in range(G):
            column = lax.broadcasted_iota(jnp.int32, (T, D), 1)
            pick = jnp.where(column == within + g * Q, 1.0, 0.0).astype(jnp.bfloat16)
            wide = lax.dot_general(rows, pick, ALONG, preferred_element_type=jnp.float32)
            for h in range(2):
                half = jnp.where(in_place, wide[h * K // 2:(h + 1) * K // 2], 0.0)
                id_rows[i * G + g, h:h + 1, :] = jnp.sum(half, axis=0, keepdims=True)
        return 0

    lax.fori_loop(0, span, partner_ids, 0)

    out_line = lax.broadcasted_iota(jnp.int32, (T, T), 0)
    spot = jnp.concatenate([lax.broadcasted_iota(jnp.int32, (T, Q), 1)] * (T // Q), axis=1)
    for h in range(2):
        for g in range(G):
            fold[h, :, g * T:(g + 1) * T] = jnp.where(
                out_line == spot * G + h * D + g, 1.0, 0.0).astype(fold.dtype)

    def arrived(slot):
        return pltpu.make_async_remote_copy(
            src_ref=buf.at[slot], dst_ref=buf.at[slot],
            send_sem=spread_sem.at[0], recv_sem=recv_sem.at[slot],
            device_id=(me, lax.rem(grp + 1, G)), device_id_type=MESH)

    def passing(i, g):
        k = grp * span + i + 1 - 2 * side
        return pltpu.make_async_remote_copy(
            src_ref=buf.at[i * G + g], dst_ref=buf.at[lax.rem(k, span) * G + g],
            send_sem=spread_sem.at[2 * levels + G + i * G + g],
            recv_sem=recv_sem.at[lax.rem(k, span) * G + g],
            device_id=(me + 1 - 2 * side, lax.div(k, span)), device_id_type=MESH)

    def passed(half, act):
        i = 2 * half

        @pl.when(grp * span + i != 0)
        def _():
            for g in range(0, G, 2):
                act(i, g)

    def pass_on(half, _):
        def act(i, g):
            arrived(i * G + g).wait_recv()
            passing(i, g).start()

        passed(half, act)
        return 0

    lax.fori_loop(0, span // 2, pass_on, 0)

    def squares_of(slot):
        total = jnp.zeros((Q, T), jnp.float32)
        for k in range(K):
            part = buf[slot, k * Q:(k + 1) * Q, :].astype(jnp.float32)
            total = total + part * part
        return total

    for g in range(G):
        @pl.when(g != grp)
        def _():
            arrived(home + g).wait_recv()

        own_norm[g * Q:(g + 1) * Q, :] = jnp.broadcast_to(
            jnp.sum(squares_of(home + g), axis=1, keepdims=True), (Q, T))

    def compare(i, _):
        k = grp * span + i
        base = jnp.where(k == 0, home, i * G)
        for g in range(G):
            @pl.when((lax.rem(k, 2) == 1) if g % 2 == 0 else (k != 0))
            def _():
                arrived(i * G + g).wait_recv()

        own = buf[home:home + G].reshape(G * K * Q, T)
        for g in range(G):
            gram = lax.dot_general(own, buf[base + g], ALONG, preferred_element_type=jnp.float32)
            theirs = [id_rows[i * G + g, h:h + 1, :] for h in range(2)]
            for e in range(G):
                sums = [jnp.zeros((Q, T), jnp.float32) for _ in range(2)]
                for j in range(K):
                    here = own_columns[j, e * Q:(e + 1) * Q, :]
                    for h in range(2):
                        part = gram[(e * K + j) * Q:(e * K + j + 1) * Q, h * T:(h + 1) * T]
                        sums[h] = sums[h] + jnp.where(here == theirs[h], part, 0.0)
                parts[i * G + g, e * Q:(e + 1) * Q, :] = sums[0] + sums[1]
            squares[pl.ds(i * D + g, Q, stride=G), :] = squares_of(base + g)
        return 0

    lax.fori_loop(0, span, compare, 0)

    def split(x):
        pieces = []
        for _ in range(3):
            pieces.append(x.astype(jnp.bfloat16))
            x = x - pieces[-1].astype(jnp.float32)
        return pieces

    ones = jnp.ones((D, T), jnp.bfloat16)
    for c in range(span * D // T):
        product = jnp.zeros((D, T), jnp.float32)
        for h in range(2):
            whole = jnp.concatenate([parts[(2 * c + h) * G + g] for g in range(G)], axis=1)
            for piece in split(whole):
                product = product + lax.dot_general(piece, fold[h], ALONG,
                                                    preferred_element_type=jnp.float32)
        rest = own_norm[...] - product
        for piece in split(squares[c * T:(c + 1) * T, :]):
            rest = rest + lax.dot_general(ones, piece, ALONG, preferred_element_type=jnp.float32)
        for g in range(G):
            num_ref[c, pl.ds(g, Q, stride=G), :] = product[g * Q:(g + 1) * Q]
            den_ref[c, pl.ds(g, Q, stride=G), :] = rest[g * Q:(g + 1) * Q]

    dealt.wait_send()
    spread(lambda copy: copy.wait_send())

    def finish(half, _):
        passed(half, lambda i, g: passing(i, g).wait_send())
        return 0

    lax.fori_loop(0, span // 2, finish, 0)


def solution(mesh):
    R, G = mesh.shape["rows"], mesh.shape["grp"]
    span = R // G

    def on_device(tile_values, tile_ids, doc_tiles, row_counts):
        cap, K, T = tile_values.shape
        A = (cap + R * G - 1) // (R * G)
        Q = DOC_DEV // G
        anywhere = pl.BlockSpec(memory_space=pl.ANY)
        vmem = pl.BlockSpec(memory_space=pltpu.VMEM)
        part = pltpu.VMEM((span * DOC_DEV // T, DOC_DEV, T), jnp.float32)
        num, den = pl.pallas_call(
            functools.partial(kernel, R, G),
            out_shape=(part, part),
            in_specs=[anywhere] * 4,
            out_specs=(vmem, vmem),
            scratch_shapes=[
                pltpu.SMEM((R,), jnp.int32),
                pltpu.SMEM((cap,), jnp.int32),
                pltpu.VMEM((K, cap), jnp.int32),
                pltpu.VMEM((cap, K, T), jnp.bfloat16),
                pltpu.VMEM((R, A + 1, K, T), jnp.bfloat16),
                pltpu.VMEM((R, A + 1, K, T), jnp.bfloat16),
                pltpu.SMEM((2, Q), jnp.int32),
                pltpu.VMEM((Q * K, T), jnp.float32),
                pltpu.VMEM(((span + 1) * G, K * Q, T), jnp.bfloat16),
                pltpu.VMEM((K, DOC_DEV, T), jnp.float32),
                pltpu.VMEM((span * G, 2, T), jnp.float32),
                pltpu.VMEM((DOC_DEV, T), jnp.float32),
                pltpu.VMEM((span * DOC_DEV, T), jnp.float32),
                pltpu.VMEM((span * G, DOC_DEV, T), jnp.float32),
                pltpu.VMEM((2, T, G * T), jnp.bfloat16),
                pltpu.SemaphoreType.DMA((4,)),
                pltpu.SemaphoreType.DMA,
                pltpu.SemaphoreType.DMA((R + G + span * G,)),
                pltpu.SemaphoreType.DMA(((span + 1) * G,)),
                pltpu.SemaphoreType.DMA,
            ],
            compiler_params=pltpu.CompilerParams(collective_id=0, has_side_effects=True),
        )(row_counts, doc_tiles, tile_ids.T, tile_values)
        return (num / den).transpose(1, 0, 2).reshape(DOC_DEV, span * DOC_DEV)

    placed = (P("rows", None, None), P("rows", None), P("rows"), P())
    return jax.shard_map(
        on_device, mesh=mesh, in_specs=placed, out_specs=P("rows", "grp"), check_vma=False
    )
```

time: 26.8 us -> 25.2 us (0.940); the launches traced: 26.4 us -> 25.1 us
  Pallas kernels: 25.7 us -> 24.4 us
    pallas_call x1, Pallas kernels: 25.7 us -> 24.4 us  [on_device(): pl.pallas_call(functools.partial(kernel, R, G), out_shape=(part, part), i...]
where the time goes in v2:
time: 25.2 us; the launch traced here: 25.1 us
  Pallas kernels  24.4 us (97%)
  other arithmetic  0.63 us (2%)
    pallas_call x1, Pallas kernels, on_device(): pl.pallas_call(functools.partial(kernel, R, G), out_shape=(part, part), i...  24.4 us
    another operation x1, other arithmetic, on_device(): return (num / den).transpose(1, 0, 2).reshape(DOC_DEV, span * DOC_DEV)  0.63 us

profile of v2, /device:TPU:1, one launch (start us, length us, event | category | flops | bytes accessed | tf_op | source)
XLA Modules:
  0.0 25.1 jit_solution(4199637343568837209)
XLA Ops:
  0.0 24.4 %shard_map.46 = (f32[1,64,128]{2,1,0:T(8,128)S(1)}, f32[1,64,128]{2,1,0:T(8,128)S(1)}) custom-call(s32[8]{0:T(128)} %counts_hbm.1, s32[128]{0:T(128)} %tiles_hbm.1, s32[16,128]{1,0:T(8,128)} %bitcast.3, bf16[128,16,128]{2,1,0:T(8,128)(2,1)} %vals_hbm.1), custom_call_target="tpu_custom_call" | custom-call | tf_op jit(solution)/shard_map/pallas_call | solution.py:331
  24.4 0.6 %divide_bitcast_fusion = f32[64,128]{1,0:T(8,128)} fusion(f32[1,64,128]{2,1,0:T(8,128)S(1)} %get-tuple-element.7, f32[1,64,128]{2,1,0:T(8,128)S(1)} %get-tuple-element.8), kind=kLoop, calls=%fused_computation | loop fusion | flops 8192 | bytes 98304 | tf_op jit(solution)/shard_map/reshape;transpose | solution.py:360

commit v3 on v2

v3 whole, which is shorter than its diff:
```python
import functools

import jax
import jax.numpy as jnp
from jax import lax
from jax.experimental import pallas as pl
from jax.experimental.pallas import tpu as pltpu
from jax.sharding import PartitionSpec as P

MESH = pl.DeviceIdType.MESH
DOC_DEV = 64
ALONG = (((1,), (1,)), ((), ()))


def kernel(R, G, counts_hbm, tiles_hbm, ids_hbm, vals_hbm, out_ref,
           counts_ref, tiles_ref, ids, vals, staged, inc, tables, place, work, near, far,
           near_ids, far_ids, squares, found, got, flat, fetch_sem, deal_send, deal_recv,
           table_send, table_recv, spread_send, near_recv, far_recv, give_send, give_recv):
    cap, K, T = vals.shape
    span = R // G
    D = DOC_DEV
    Q = D // G
    A = staged.shape[1]
    me = lax.axis_index("rows")
    grp = lax.axis_index("grp")
    peer = grp + 1 - 2 * lax.rem(grp, 2)
    share = span // 2
    levels = R // 2
    level = lax.div(me, 2)
    side = lax.rem(me, 2)
    seat = side * G + grp

    fetches = [
        pltpu.make_async_copy(src, dst, fetch_sem.at[n])
        for n, (src, dst) in enumerate(
            ((vals_hbm, vals), (ids_hbm, ids), (counts_hbm, counts_ref), (tiles_hbm, tiles_ref)))
    ]
    for fetch in fetches:
        fetch.start()

    barrier = pltpu.get_barrier_semaphore()

    def greet(row, g):
        pl.semaphore_signal(barrier, inc=1, device_id=(row, g), device_id_type=MESH)

    def greet_row(d, _):
        greet(lax.rem(me + d, R), peer)
        return 0

    lax.fori_loop(1, R, greet_row, 0)
    for e in range(1, G):
        greet(me, lax.rem(grp + e, G))

    for fetch in fetches[1:]:
        fetch.wait()

    def add_up(r, total):
        return total + jnp.where(r < me, counts_ref[r], 0)

    start = lax.fori_loop(0, R, add_up, jnp.int32(0), unroll=R <= 8)
    tile_line = lax.broadcasted_iota(jnp.int32, (K, T), 0)
    tables[me] = ids[...].astype(jnp.float32).astype(tables.dtype)
    fetches[0].wait()

    def stage(b, _):
        lag = lax.rem(start, R * G)
        first = lax.rem(b + R * jnp.where(b == me, grp, peer) + R * G - lag, R * G)
        for a in range(A):
            s = jnp.minimum(first + a * R * G, cap - 1)
            block = vals[s].astype(jnp.float32)
            block = jnp.where(tile_line < tiles_ref[s], block, 0.0)
            staged[b, a] = block.astype(staged.dtype)
        return 0

    lax.fori_loop(0, R, stage, 0)
    pl.semaphore_wait(barrier, R - 1 + G - 1)

    def far_first(n, at, size):
        near = jnp.minimum(at, size - 1 - at)
        m = n - jnp.abs(size - 1 - 2 * at)
        up = jnp.where(m < 0, 2 * at < size, lax.rem(m, 2) == 0)
        away = jnp.where(m < 0, near - m, near - lax.div(m, 2))
        return at + jnp.where(up, away, -away)

    def deal(n, _):
        row = far_first(n, me, R)
        pltpu.make_async_remote_copy(
            src_ref=staged.at[row], dst_ref=inc.at[me],
            send_sem=deal_send, recv_sem=deal_recv,
            device_id=(row, peer), device_id_type=MESH).start()
        return 0

    lax.fori_loop(0, R - 1, deal, 0)

    def tell(n, _):
        pltpu.make_async_remote_copy(
            src_ref=tables.at[me], dst_ref=tables.at[me],
            send_sem=table_send, recv_sem=table_recv,
            device_id=(far_first(n, me, R), peer), device_id_type=MESH).start()
        return 0

    lax.fori_loop(0, R - 1, tell, 0)
    inc[me] = staged[me]

    def source_of(g):
        def look(r, carry):
            end, behind, begin = carry
            end = end + counts_ref[r]
            past = g >= end
            return (end, behind + jnp.where(past, 1, 0), jnp.where(past, end, begin))

        zero = jnp.int32(0)
        _, source, begin = lax.fori_loop(0, R, look, (zero, zero, zero), unroll=R <= 8)
        return jnp.minimum(source, R - 1), jnp.minimum(lax.div(g - begin, R * G), A - 1)

    def note(j, _):
        source, a = source_of((j * G + grp) * R + me)
        place[0, j] = source
        place[1, j] = a
        return 0

    lax.fori_loop(0, Q, note, 0)

    dealt = pltpu.make_async_remote_copy(
        src_ref=staged.at[pl.ds(0, R - 1)], dst_ref=inc.at[pl.ds(0, R - 1)],
        send_sem=deal_send, recv_sem=deal_recv,
        device_id=(me, lax.rem(grp + 1, G)), device_id_type=MESH)
    dealt.wait_recv()

    def bring(j, _):
        work[pl.ds(pl.multiple_of(j * K, K), K), :] = inc[place[0, j], place[1, j]].astype(jnp.float32)
        return 0

    lax.fori_loop(0, Q, bring, 0, unroll=8)
    for k in range(K):
        part = work[pl.ds(k, Q, stride=K), :].astype(near.dtype)
        near[seat, k * Q:(k + 1) * Q, :] = part
        far[0, k * Q:(k + 1) * Q, :] = part

    def mate(e):
        other = lax.rem(seat + e, 2 * G)
        return 2 * level + lax.div(other, G), lax.rem(other, G)

    def cousin(e):
        return lax.rem(seat + 2 * e, 2 * G)

    def to_mate(e):
        other = cousin(e)
        row = jnp.where(e == 0, me, 2 * level + lax.div(other, G))
        return pltpu.make_async_remote_copy(
            src_ref=far.at[0], dst_ref=near.at[seat],
            send_sem=spread_send.at[e], recv_sem=near_recv.at[seat],
            device_id=(row, jnp.where(e == 0, peer, lax.rem(other, G))), device_id_type=MESH)

    def pass_on(e):
        return pltpu.make_async_remote_copy(
            src_ref=near.at[cousin(e)], dst_ref=near.at[cousin(e)],
            send_sem=spread_send.at[G + e], recv_sem=near_recv.at[cousin(e)],
            device_id=(me, peer), device_id_type=MESH)

    def to_level(n):
        there = far_first(n, level, levels)
        lag = lax.rem(there + levels - level, levels)
        return pltpu.make_async_remote_copy(
            src_ref=far.at[0], dst_ref=far.at[lag],
            send_sem=spread_send.at[2 * G + n], recv_sem=far_recv.at[lag],
            device_id=(2 * there + side, grp), device_id_type=MESH)

    def spread(act):
        def each(n, _):
            act(to_level(n))
            return 0

        lax.fori_loop(0, levels - 1, each, 0)
        for e in range(G):
            act(to_mate(e))

    spread(lambda copy: copy.start())

    told = pltpu.make_async_remote_copy(
        src_ref=tables.at[pl.ds(0, R - 1)], dst_ref=tables.at[pl.ds(0, R - 1)],
        send_sem=table_send, recv_sem=table_recv,
        device_id=(me, lax.rem(grp + 1, G)), device_id_type=MESH)
    told.wait_recv()
    lane = lax.broadcasted_iota(jnp.int32, (1, T), 1)
    step = lax.broadcasted_iota(jnp.int32, (Q, T), 0) * (G * R)
    near_line = jnp.concatenate(
        [step + g * R + 2 * level + x for x in range(2) for g in range(G)], axis=0)
    far_line = jnp.concatenate(
        [step + grp * R + 2 * lax.rem(level + levels - lag, levels) + side
         for lag in range(levels)], axis=0)

    def look_up(r, carry):
        begin, rows, columns = carry
        line = jnp.where(lane < counts_ref[r], begin + lane, -1)
        near_hot = jnp.where(near_line == line, 1.0, 0.0).astype(jnp.bfloat16)
        far_hot = jnp.where(far_line == line, 1.0, 0.0).astype(jnp.bfloat16)
        rows = rows + lax.dot_general(tables[r], near_hot, ALONG,
                                      preferred_element_type=jnp.float32)
        columns = columns + lax.dot_general(far_hot, tables[r], ALONG,
                                            preferred_element_type=jnp.float32)
        return begin + counts_ref[r], rows, columns

    nothing = (jnp.int32(0), jnp.zeros((K, T), jnp.float32),
               jnp.zeros((levels * Q, K), jnp.float32))
    _, rows, columns = lax.fori_loop(0, R, look_up, nothing, unroll=R <= 8)
    near_ids[...] = rows
    for k in range(K):
        far_ids[k] = jnp.broadcast_to(columns[:, k:k + 1], (levels * Q, T))

    def squares_of(ref, slot):
        total = jnp.zeros((Q, T), jnp.float32)
        for k in range(K):
            part = ref[slot, k * Q:(k + 1) * Q, :].astype(jnp.float32)
            total = total + part * part
        return total

    def split(x):
        pieces = []
        for _ in range(3):
            pieces.append(x.astype(jnp.bfloat16))
            x = x - pieces[-1].astype(jnp.float32)
        return pieces

    def landed(slot):
        pltpu.make_async_remote_copy(
            src_ref=far.at[0], dst_ref=near.at[slot],
            send_sem=spread_send.at[0], recv_sem=near_recv.at[slot],
            device_id=(me, peer), device_id_type=MESH).wait_recv()

    for e in range(1, G):
        landed(cousin(e))
        pass_on(e).start()
    for e in range(G):
        landed(lax.rem(peer + side * G + 2 * e, 2 * G))

    for slot in range(2 * G):
        squares[slot * Q:(slot + 1) * Q, :] = squares_of(near, slot)

    ones = jnp.ones((Q, T), jnp.bfloat16)
    near_norm = jnp.zeros((Q, T), jnp.float32)
    for piece in split(squares[...]):
        near_norm = near_norm + lax.dot_general(ones, piece, ALONG,
                                                preferred_element_type=jnp.float32)

    def compare(group, _):
        rows = far[pl.ds(group * batch, batch)].reshape(batch * K * Q, T)
        sums = [[jnp.zeros((Q, T), jnp.float32) for _ in range(2)] for _ in range(batch)]
        for p in range(K // 2):
            block = jnp.concatenate(
                [near[slot, k * Q:(k + 1) * Q, :]
                 for k in (2 * p, 2 * p + 1) for slot in range(2 * G)], axis=0)
            gram = lax.dot_general(rows, block, ALONG, preferred_element_type=jnp.float32)
            theirs = [near_ids[2 * p + h:2 * p + h + 1, :] for h in range(2)]
            for b in range(batch):
                for k in range(K):
                    first = pl.multiple_of((group * batch + b) * Q, Q)
                    here = far_ids[k, pl.ds(first, Q), :]
                    for h in range(2):
                        part = gram[(b * K + k) * Q:(b * K + k + 1) * Q, h * T:(h + 1) * T]
                        sums[b][h] = sums[b][h] + jnp.where(here == theirs[h], part, 0.0)
        for b in range(batch):
            lag = group * batch + b
            product = sums[b][0] + sums[b][1]
            norm = jnp.sum(squares_of(far, lag), axis=1, keepdims=True)
            found[lag] = product / (near_norm + norm - product)
        return 0

    dealt.wait_send()
    told.wait_send()
    spread(lambda copy: copy.wait_send())

    def visit(lag, _):
        pltpu.make_async_remote_copy(
            src_ref=far.at[0], dst_ref=far.at[lag],
            send_sem=spread_send.at[0], recv_sem=far_recv.at[lag],
            device_id=mate(1), device_id_type=MESH).wait_recv()
        return 0

    lax.fori_loop(1, levels, visit, 0)
    batch = min(levels, 4)
    lax.fori_loop(0, levels // batch, compare, 0)
    found[levels] = found[0]

    def give(e):
        row, g = mate(e)
        turned = side * jnp.abs(lax.rem(row, 2) - side)
        return pltpu.make_async_remote_copy(
            src_ref=found.at[pl.ds(g * share + turned, share)], dst_ref=got.at[seat],
            send_sem=give_send.at[e], recv_sem=give_recv.at[seat],
            device_id=(row, g), device_id_type=MESH)

    for e in range(1, 2 * G):
        give(e).start()
    got[seat] = found[pl.ds(grp * share, share)]

    for slot in range(2 * G):
        @pl.when(slot != seat)
        def _():
            pltpu.make_async_remote_copy(
                src_ref=found.at[pl.ds(0, share)], dst_ref=got.at[slot],
                send_sem=give_send.at[0], recv_sem=give_recv.at[slot],
                device_id=mate(1), device_id_type=MESH).wait_recv()

        for s in range(share):
            i = 2 * s + jnp.abs(slot // G - side)
            flat[pl.ds(i * D + slot % G, Q, stride=G), :] = got[slot, s]

    across = flat[...].T
    across = jnp.where(side == 0, across[:D], across[D:])
    for g in range(G):
        for c in range(span * D // T):
            out_ref[c, pl.ds(g, Q, stride=G), :] = across[g * Q:(g + 1) * Q, c * T:(c + 1) * T]

    for e in range(1, G):
        pass_on(e).wait_send()
    for e in range(1, 2 * G):
        give(e).wait_send()


def solution(mesh):
    R, G = mesh.shape["rows"], mesh.shape["grp"]
    span = R // G

    def on_device(tile_values, tile_ids, doc_tiles, row_counts):
        cap, K, T = tile_values.shape
        A = (cap + R * G - 1) // (R * G)
        Q = DOC_DEV // G
        chunks = span * DOC_DEV // T
        anywhere = pl.BlockSpec(memory_space=pl.ANY)
        dma = pltpu.SemaphoreType.DMA
        out = pl.pallas_call(
            functools.partial(kernel, R, G),
            out_shape=pltpu.VMEM((chunks, DOC_DEV, T), jnp.float32),
            in_specs=[anywhere] * 4,
            out_specs=pl.BlockSpec(memory_space=pltpu.VMEM),
            scratch_shapes=[
                pltpu.SMEM((R,), jnp.int32),
                pltpu.SMEM((cap,), jnp.int32),
                pltpu.VMEM((K, cap), jnp.int32),
                pltpu.VMEM((cap, K, T), jnp.bfloat16),
                pltpu.VMEM((R, A, K, T), jnp.bfloat16),
                pltpu.VMEM((R, A, K, T), jnp.bfloat16),
                pltpu.VMEM((R, K, T), jnp.bfloat16),
                pltpu.SMEM((2, Q), jnp.int32),
                pltpu.VMEM((Q * K, T), jnp.float32),
                pltpu.VMEM((2 * G, K * Q, T), jnp.bfloat16),
                pltpu.VMEM((R // 2, K * Q, T), jnp.bfloat16),
                pltpu.VMEM((K, T), jnp.float32),
                pltpu.VMEM((K, R // 2 * Q, T), jnp.float32),
                pltpu.VMEM((2 * G * Q, T), jnp.float32),
                pltpu.VMEM((R // 2 + 1, Q, T), jnp.float32),
                pltpu.VMEM((2 * G, span // 2, Q, T), jnp.float32),
                pltpu.VMEM((span * DOC_DEV, T), jnp.float32),
                dma((4,)), dma, dma, dma, dma, dma((2 * G + R // 2,)), dma((2 * G,)),
                dma((R // 2,)), dma((2 * G,)), dma((2 * G,)),
            ],
            compiler_params=pltpu.CompilerParams(collective_id=0, has_side_effects=True),
        )(row_counts, doc_tiles, tile_ids.T, tile_values)
        return out.transpose(1, 0, 2).reshape(DOC_DEV, span * DOC_DEV)

    placed = (P("rows", None, None), P("rows", None), P("rows"), P())
    return jax.shard_map(
        on_device, mesh=mesh, in_specs=placed, out_specs=P("rows", "grp"), check_vma=False
    )
```

time: 25.2 us -> 23.5 us (0.933)
  the two profiles are of different devices: /device:TPU:1 before, /device:TPU:0 now
where the time goes in v3:
time: 23.5 us; the launch traced here: 23.4 us
  Pallas kernels  22.8 us (97%)
  local copies, waits for them, and re-layouts  0.62 us (3%)
    pallas_call x1, Pallas kernels, on_device(): pl.pallas_call(functools.partial(kernel, R, G), out_shape=pltpu.VMEM((chu...  22.8 us
    unnamed x1, local copies, waits for them, and re-layouts  0.62 us

profile of v3, /device:TPU:0, one launch (start us, length us, event | category | flops | bytes accessed | tf_op | source)
XLA Modules:
  0.0 23.4 jit_solution(15508928810724222983)
XLA Ops:
  0.0 22.8 %shard_map.46 = f32[1,64,128]{2,1,0:T(8,128)S(1)} custom-call(s32[8]{0:T(128)} %counts_hbm.1, s32[128]{0:T(128)} %tiles_hbm.1, s32[16,128]{1,0:T(8,128)} %bitcast.3, bf16[128,16,128]{2,1,0:T(8,128)(2,1)} %vals_hbm.1), custom_call_target="tpu_custom_call" | custom-call | tf_op jit(solution)/shard_map/pallas_call | solution.py:332
  22.8 0.6 %copy.6 = f32[64,128]{1,0:T(8,128)} copy(f32[64,128]{1,0:T(8,128)S(1)} %bitcast.2) | data formatting | bytes 65536

commit v4 on v3

--- a/solution.py
+++ b/solution.py
@@ -15,7 +15,8 @@
 def kernel(R, G, counts_hbm, tiles_hbm, ids_hbm, vals_hbm, out_ref,
            counts_ref, tiles_ref, ids, vals, staged, inc, tables, place, work, near, far,
            near_ids, far_ids, squares, found, got, flat, fetch_sem, deal_send, deal_recv,
-           table_send, table_recv, spread_send, near_recv, far_recv, give_send, give_recv):
+           table_send, table_recv, level_send, far_recv, mate_send, pass_send, near_recv,
+           give_send, give_recv):
     cap, K, T = vals.shape
     span = R // G
     D = DOC_DEV
@@ -78,12 +79,16 @@
     def far_first(n, at, size):
         near = jnp.minimum(at, size - 1 - at)
         m = n - jnp.abs(size - 1 - 2 * at)
-        up = jnp.where(m < 0, 2 * at < size, lax.rem(m, 2) == 0)
+        up = jnp.where(m < 0, 2 * at < size, lax.rem(n, 2) == 0)
         away = jnp.where(m < 0, near - m, near - lax.div(m, 2))
         return at + jnp.where(up, away, -away)
 
+    def farthest(n):
+        there = jnp.where(n == R - 2, level, far_first(lax.div(n, 2), level, levels))
+        return 2 * there + jnp.where(lax.rem(n, 2) == 0, 1 - side, side)
+
     def deal(n, _):
-        row = far_first(n, me, R)
+        row = farthest(n)
         pltpu.make_async_remote_copy(
             src_ref=staged.at[row], dst_ref=inc.at[me],
             send_sem=deal_send, recv_sem=deal_recv,
@@ -96,7 +101,7 @@
         pltpu.make_async_remote_copy(
             src_ref=tables.at[me], dst_ref=tables.at[me],
             send_sem=table_send, recv_sem=table_recv,
-            device_id=(far_first(n, me, R), peer), device_id_type=MESH).start()
+            device_id=(farthest(n), peer), device_id_type=MESH).start()
         return 0
 
     lax.fori_loop(0, R - 1, tell, 0)
@@ -144,18 +149,20 @@
     def cousin(e):
         return lax.rem(seat + 2 * e, 2 * G)
 
+    def flip(slot):
+        return slot + 1 - 2 * lax.rem(slot, 2)
+
     def to_mate(e):
-        other = cousin(e)
-        row = jnp.where(e == 0, me, 2 * level + lax.div(other, G))
+        other = flip(cousin(e))
         return pltpu.make_async_remote_copy(
             src_ref=far.at[0], dst_ref=near.at[seat],
-            send_sem=spread_send.at[e], recv_sem=near_recv.at[seat],
-            device_id=(row, jnp.where(e == 0, peer, lax.rem(other, G))), device_id_type=MESH)
+            send_sem=mate_send, recv_sem=near_recv.at[lax.rem(G - e, G)],
+            device_id=(2 * level + lax.div(other, G), lax.rem(other, G)), device_id_type=MESH)
 
     def pass_on(e):
         return pltpu.make_async_remote_copy(
-            src_ref=near.at[cousin(e)], dst_ref=near.at[cousin(e)],
-            send_sem=spread_send.at[G + e], recv_sem=near_recv.at[cousin(e)],
+            src_ref=near.at[flip(cousin(e))], dst_ref=near.at[flip(cousin(e))],
+            send_sem=pass_send, recv_sem=near_recv.at[0],
             device_id=(me, peer), device_id_type=MESH)
 
     def to_level(n):
@@ -163,31 +170,31 @@
         lag = lax.rem(there + levels - level, levels)
         return pltpu.make_async_remote_copy(
             src_ref=far.at[0], dst_ref=far.at[lag],
-            send_sem=spread_send.at[2 * G + n], recv_sem=far_recv.at[lag],
-            device_id=(2 * there + side, grp), device_id_type=MESH)
-
-    def spread(act):
-        def each(n, _):
-            act(to_level(n))
-            return 0
-
-        lax.fori_loop(0, levels - 1, each, 0)
-        for e in range(G):
-            act(to_mate(e))
-
-    spread(lambda copy: copy.start())
-
-    told = pltpu.make_async_remote_copy(
-        src_ref=tables.at[pl.ds(0, R - 1)], dst_ref=tables.at[pl.ds(0, R - 1)],
-        send_sem=table_send, recv_sem=table_recv,
-        device_id=(me, lax.rem(grp + 1, G)), device_id_type=MESH)
+            send_sem=level_send, recv_sem=far_recv.at[lag],
+            device_id=(2 * there + side, peer), device_id_type=MESH)
+
+    def spread(n, _):
+        to_level(n).start()
+        return 0
+
+    lax.fori_loop(0, levels - 1, spread, 0)
+    for e in range(G):
+        to_mate(e).start()
+
+    def bulk(ref, first, amount, send, recv):
+        part = ref.at[pl.ds(first, amount)]
+        return pltpu.make_async_remote_copy(
+            src_ref=part, dst_ref=part, send_sem=send, recv_sem=recv,
+            device_id=(me, peer), device_id_type=MESH)
+
+    told = bulk(tables, 0, R - 1, table_send, table_recv)
     told.wait_recv()
     lane = lax.broadcasted_iota(jnp.int32, (1, T), 1)
     step = lax.broadcasted_iota(jnp.int32, (Q, T), 0) * (G * R)
     near_line = jnp.concatenate(
         [step + g * R + 2 * level + x for x in range(2) for g in range(G)], axis=0)
     far_line = jnp.concatenate(
-        [step + grp * R + 2 * lax.rem(level + levels - lag, levels) + side
+        [step + (peer if lag else grp) * R + 2 * lax.rem(level + levels - lag, levels) + side
          for lag in range(levels)], axis=0)
 
     def look_up(r, carry):
@@ -222,17 +229,10 @@
             x = x - pieces[-1].astype(jnp.float32)
         return pieces
 
-    def landed(slot):
-        pltpu.make_async_remote_copy(
-            src_ref=far.at[0], dst_ref=near.at[slot],
-            send_sem=spread_send.at[0], recv_sem=near_recv.at[slot],
-            device_id=(me, peer), device_id_type=MESH).wait_recv()
-
     for e in range(1, G):
-        landed(cousin(e))
+        bulk(near, flip(cousin(e)), 1, mate_send, near_recv.at[e]).wait_recv()
         pass_on(e).start()
-    for e in range(G):
-        landed(lax.rem(peer + side * G + 2 * e, 2 * G))
+    bulk(near, 0, G, mate_send, near_recv.at[0]).wait_recv()
 
     for slot in range(2 * G):
         squares[slot * Q:(slot + 1) * Q, :] = squares_of(near, slot)
@@ -243,43 +243,44 @@
         near_norm = near_norm + lax.dot_general(ones, piece, ALONG,
                                                 preferred_element_type=jnp.float32)
 
-    def compare(group, _):
-        rows = far[pl.ds(group * batch, batch)].reshape(batch * K * Q, T)
-        sums = [[jnp.zeros((Q, T), jnp.float32) for _ in range(2)] for _ in range(batch)]
+    def compare(lags):
+        sums = [[jnp.zeros((Q, T), jnp.float32) for _ in range(4)] for _ in lags]
         for p in range(K // 2):
             block = jnp.concatenate(
                 [near[slot, k * Q:(k + 1) * Q, :]
                  for k in (2 * p, 2 * p + 1) for slot in range(2 * G)], axis=0)
-            gram = lax.dot_general(rows, block, ALONG, preferred_element_type=jnp.float32)
             theirs = [near_ids[2 * p + h:2 * p + h + 1, :] for h in range(2)]
-            for b in range(batch):
+            for lag, chains in zip(lags, sums):
+                gram = lax.dot_general(far[lag], block, ALONG, preferred_element_type=jnp.float32)
                 for k in range(K):
-                    first = pl.multiple_of((group * batch + b) * Q, Q)
-                    here = far_ids[k, pl.ds(first, Q), :]
+                    here = far_ids[k, pl.ds(pl.multiple_of(lag * Q, Q), Q), :]
                     for h in range(2):
-                        part = gram[(b * K + k) * Q:(b * K + k + 1) * Q, h * T:(h + 1) * T]
-                        sums[b][h] = sums[b][h] + jnp.where(here == theirs[h], part, 0.0)
-        for b in range(batch):
-            lag = group * batch + b
-            product = sums[b][0] + sums[b][1]
+                        part = gram[k * Q:(k + 1) * Q, h * T:(h + 1) * T]
+                        c = 2 * h + k % 2
+                        chains[c] = chains[c] + jnp.where(here == theirs[h], part, 0.0)
+        for lag, chains in zip(lags, sums):
+            product = (chains[0] + chains[1]) + (chains[2] + chains[3])
             norm = jnp.sum(squares_of(far, lag), axis=1, keepdims=True)
             found[lag] = product / (near_norm + norm - product)
-        return 0
 
     dealt.wait_send()
     told.wait_send()
-    spread(lambda copy: copy.wait_send())
-
-    def visit(lag, _):
-        pltpu.make_async_remote_copy(
-            src_ref=far.at[0], dst_ref=far.at[lag],
-            send_sem=spread_send.at[0], recv_sem=far_recv.at[lag],
-            device_id=mate(1), device_id_type=MESH).wait_recv()
-        return 0
-
-    lax.fori_loop(1, levels, visit, 0)
-    batch = min(levels, 4)
-    lax.fori_loop(0, levels // batch, compare, 0)
+    bulk(near, 0, G, mate_send, near_recv.at[0]).wait_send()
+    bulk(far, 1, levels - 1, level_send, far_recv.at[0]).wait_send()
+
+    def visitor(n):
+        there = far_first(n, level, levels)
+        lag = lax.rem(level + levels - there, levels)
+        bulk(far, lag, 1, level_send, far_recv.at[lag]).wait_recv()
+        return lag
+
+    compare([0, visitor(levels - 2)])
+
+    def visit(n, _):
+        compare([visitor(levels - 3 - 2 * n), visitor(levels - 4 - 2 * n)])
+        return 0
+
+    lax.fori_loop(0, (levels - 2) // 2, visit, 0)
     found[levels] = found[0]
 
     def give(e):
@@ -287,35 +288,29 @@
         turned = side * jnp.abs(lax.rem(row, 2) - side)
         return pltpu.make_async_remote_copy(
             src_ref=found.at[pl.ds(g * share + turned, share)], dst_ref=got.at[seat],
-            send_sem=give_send.at[e], recv_sem=give_recv.at[seat],
+            send_sem=give_send, recv_sem=give_recv,
             device_id=(row, g), device_id_type=MESH)
 
     for e in range(1, 2 * G):
         give(e).start()
     got[seat] = found[pl.ds(grp * share, share)]
+    bulk(near, 0, G - 1, pass_send, near_recv.at[0]).wait_send()
+    given = bulk(got, 0, 2 * G - 1, give_send, give_recv)
+    given.wait_send()
+    given.wait_recv()
 
     for slot in range(2 * G):
-        @pl.when(slot != seat)
-        def _():
-            pltpu.make_async_remote_copy(
-                src_ref=found.at[pl.ds(0, share)], dst_ref=got.at[slot],
-                send_sem=give_send.at[0], recv_sem=give_recv.at[slot],
-                device_id=mate(1), device_id_type=MESH).wait_recv()
-
+        crossed = jnp.abs(slot // G - side)
         for s in range(share):
-            i = 2 * s + jnp.abs(slot // G - side)
-            flat[pl.ds(i * D + slot % G, Q, stride=G), :] = got[slot, s]
+            lag = lax.rem(grp * share + s + slot // G * crossed, levels)
+            quarter = jnp.where(lag == 0, slot % G, slot % G + 1 - 2 * (slot % 2))
+            flat[pl.ds((2 * s + crossed) * D + quarter, Q, stride=G), :] = got[slot, s]
 
     across = flat[...].T
     across = jnp.where(side == 0, across[:D], across[D:])
     for g in range(G):
         for c in range(span * D // T):
             out_ref[c, pl.ds(g, Q, stride=G), :] = across[g * Q:(g + 1) * Q, c * T:(c + 1) * T]
-
-    for e in range(1, G):
-        pass_on(e).wait_send()
-    for e in range(1, 2 * G):
-        give(e).wait_send()
 
 
 def solution(mesh):
@@ -352,8 +347,7 @@
                 pltpu.VMEM((R // 2 + 1, Q, T), jnp.float32),
                 pltpu.VMEM((2 * G, span // 2, Q, T), jnp.float32),
                 pltpu.VMEM((span * DOC_DEV, T), jnp.float32),
-                dma((4,)), dma, dma, dma, dma, dma((2 * G + R // 2,)), dma((2 * G,)),
-                dma((R // 2,)), dma((2 * G,)), dma((2 * G,)),
+                dma((4,)), dma, dma, dma, dma, dma, dma((R // 2,)), dma, dma, dma((G,)), dma, dma,
             ],
             compiler_params=pltpu.CompilerParams(collective_id=0, has_side_effects=True),
         )(row_counts, doc_tiles, tile_ids.T, tile_values)

time: 23.5 us -> 22.3 us (0.949)
  Pallas kernels: 22.8 us -> 21.6 us
    pallas_call x1, Pallas kernels: 22.8 us -> 21.6 us  [on_device(): pl.pallas_call(functools.partial(kernel, R, G), out_shape=pltpu.VMEM((chu...]
where the time goes in v4:
time: 22.3 us; the launch traced here: 22.2 us
  Pallas kernels  21.6 us (97%)
  local copies, waits for them, and re-layouts  0.62 us (3%)
    pallas_call x1, Pallas kernels, on_device(): pl.pallas_call(functools.partial(kernel, R, G), out_shape=pltpu.VMEM((chu...  21.6 us
    unnamed x1, local copies, waits for them, and re-layouts  0.62 us

profile of v4, /device:TPU:0, one launch (start us, length us, event | category | flops | bytes accessed | tf_op | source)
XLA Modules:
  0.0 22.2 jit_solution(2067984360915016940)
XLA Ops:
  0.0 21.6 %shard_map.46 = f32[1,64,128]{2,1,0:T(8,128)S(1)} custom-call(s32[8]{0:T(128)} %counts_hbm.1, s32[128]{0:T(128)} %tiles_hbm.1, s32[16,128]{1,0:T(8,128)} %bitcast.3, bf16[128,16,128]{2,1,0:T(8,128)(2,1)} %vals_hbm.1), custom_call_target="tpu_custom_call" | custom-call | tf_op jit(solution)/shard_map/pallas_call | solution.py:327
  21.6 0.6 %copy.6 = f32[64,128]{1,0:T(8,128)} copy(f32[64,128]{1,0:T(8,128)S(1)} %bitcast.2) | data formatting | bytes 65536

commit v5 on v4

--- a/solution.py
+++ b/solution.py
@@ -232,18 +232,19 @@
     for e in range(1, G):
         bulk(near, flip(cousin(e)), 1, mate_send, near_recv.at[e]).wait_recv()
         pass_on(e).start()
+
+    def square(slot):
+        squares[pl.ds(pl.multiple_of(slot * Q, Q), Q), :] = squares_of(near, slot)
+
+    square(seat)
+    for e in range(1, G):
+        square(flip(cousin(e)))
     bulk(near, 0, G, mate_send, near_recv.at[0]).wait_recv()
-
-    for slot in range(2 * G):
-        squares[slot * Q:(slot + 1) * Q, :] = squares_of(near, slot)
-
-    ones = jnp.ones((Q, T), jnp.bfloat16)
-    near_norm = jnp.zeros((Q, T), jnp.float32)
-    for piece in split(squares[...]):
-        near_norm = near_norm + lax.dot_general(ones, piece, ALONG,
-                                                preferred_element_type=jnp.float32)
-
-    def compare(lags):
+    square(flip(seat))
+    for e in range(1, G):
+        square(cousin(e))
+
+    def compare(lags, near_norm):
         sums = [[jnp.zeros((Q, T), jnp.float32) for _ in range(4)] for _ in lags]
         for p in range(K // 2):
             block = jnp.concatenate(
@@ -274,25 +275,41 @@
         bulk(far, lag, 1, level_send, far_recv.at[lag]).wait_recv()
         return lag
 
-    compare([0, visitor(levels - 2)])
-
-    def visit(n, _):
-        compare([visitor(levels - 3 - 2 * n), visitor(levels - 4 - 2 * n)])
-        return 0
-
-    lax.fori_loop(0, (levels - 2) // 2, visit, 0)
+    distant = visitor(0)
+    ones = jnp.ones((Q, T), jnp.bfloat16)
+    near_norm = jnp.zeros((Q, T), jnp.float32)
+    for piece in split(squares[...]):
+        near_norm = near_norm + lax.dot_general(ones, piece, ALONG,
+                                                preferred_element_type=jnp.float32)
+
+    compare([0, distant], near_norm)
     found[levels] = found[0]
 
-    def give(e):
+    def give(e, when):
         row, g = mate(e)
-        turned = side * jnp.abs(lax.rem(row, 2) - side)
-        return pltpu.make_async_remote_copy(
-            src_ref=found.at[pl.ds(g * share + turned, share)], dst_ref=got.at[seat],
+        first = g * share + side * jnp.abs(lax.rem(row, 2) - side)
+        copy = pltpu.make_async_remote_copy(
+            src_ref=found.at[pl.ds(first, share)], dst_ref=got.at[seat],
             send_sem=give_send, recv_sem=give_recv,
             device_id=(row, g), device_id_type=MESH)
 
+        @pl.when(when(first))
+        def _():
+            copy.start()
+
+    def is_early(first):
+        return (share == 1) & ((lax.rem(first, levels) == 0) | (first == distant))
+
     for e in range(1, 2 * G):
-        give(e).start()
+        give(e, is_early)
+
+    def visit(n, _):
+        compare([visitor(1 + 2 * n), visitor(2 + 2 * n)], near_norm)
+        return 0
+
+    lax.fori_loop(0, (levels - 2) // 2, visit, 0)
+    for e in range(1, 2 * G):
+        give(e, lambda first: jnp.logical_not(is_early(first)))
     got[seat] = found[pl.ds(grp * share, share)]
     bulk(near, 0, G - 1, pass_send, near_recv.at[0]).wait_send()
     given = bulk(got, 0, 2 * G - 1, give_send, give_recv)

time: 22.3 us -> 21.7 us (0.973)
  the two profiles are of different devices: /device:TPU:0 before, /device:TPU:1 now
where the time goes in v5:
time: 21.7 us; the launch traced here: 21.5 us
  Pallas kernels  20.9 us (96%)
  local copies, waits for them, and re-layouts  0.62 us (3%)
    pallas_call x1, Pallas kernels, on_device(): pl.pallas_call(functools.partial(kernel, R, G), out_shape=pltpu.VMEM((chu...  20.9 us
    unnamed x1, local copies, waits for them, and re-layouts  0.62 us

profile of v5, /device:TPU:1, one launch (start us, length us, event | category | flops | bytes accessed | tf_op | source)
XLA Modules:
  0.0 21.5 jit_solution(17894867228850972320)
XLA Ops:
  0.0 20.9 %shard_map.46 = f32[1,64,128]{2,1,0:T(8,128)S(1)} custom-call(s32[8]{0:T(128)} %counts_hbm.1, s32[128]{0:T(128)} %tiles_hbm.1, s32[16,128]{1,0:T(8,128)} %bitcast.3, bf16[128,16,128]{2,1,0:T(8,128)(2,1)} %vals_hbm.1), custom_call_target="tpu_custom_call" | custom-call | tf_op jit(solution)/shard_map/pallas_call | solution.py:344
  20.9 0.6 %copy.6 = f32[64,128]{1,0:T(8,128)} copy(f32[64,128]{1,0:T(8,128)S(1)} %bitcast.2) | data formatting | bytes 65536
